TPU v7x, 32 devices: a whole 2x2x4 slice. The times are simulated.
32 devices in a mesh: dp: 8 (over z, core), tensor: 4 (over y, x).
Axes of the slice: x: 2, y: 2, z: 4, core: 2. Of those that a mesh axis runs over, the one named last changes fastest.
Arguments:
- hidden_in: bfloat16 [8192, 5120], P(('dp', 'tensor')), may hold values from -64 to 64
- q_weight: bfloat16 [5120, 1024], P('dp', 'tensor'), may hold values from -0.69877124 to 0.69877124
- k_weight: bfloat16 [5120, 1024], P('dp'), may hold values from -0.69877124 to 0.69877124
- v_weight: bfloat16 [5120, 1024], P('dp'), may hold values from -0.078125 to 0.078125
- q_gain: float32 [1024], P('tensor'), may hold values from 0.1 to 1.9
- k_gain: float32 [1024], replicated, may hold values from 0.1 to 1.9
- o_weight: bfloat16 [1024, 5120], P('tensor', 'dp'), may hold values from -0.1875 to 0.1875
- post_gain: float32 [5120], replicated, may hold values from 0.1 to 1.9
Outputs:
- layer_out: bfloat16 [8192, 5120], P(('dp', 'tensor'))
All inputs are finite; a program needn't handle non-finite values.
Results may differ from a plain program's by a relative error of at most 0.012.
Values may be sent and summed in bfloat16 or wider, within the bound.
A program may use at most 128 MiB of HBM per device.

v0:
```python
import jax
import jax.numpy as jnp
from jax import lax
from jax.sharding import PartitionSpec as P

HD = 128
KV_HEADS = 8


epsilon = 1e-06


def local(hidden_in, q_weight, k_weight, v_weight, q_gain, k_gain, o_weight, post_gain):
    heads_dev = q_weight.shape[1] // HD
    tensor_size = lax.axis_size("tensor")
    heads_all = heads_dev * tensor_size
    group_size = heads_all // KV_HEADS
    kv_count = max(1, heads_dev // group_size)
    kv_first = lax.axis_index("tensor") * heads_dev // group_size
    k_share = min(1.0, heads_dev / group_size)
    q_width = heads_dev * HD
    kv_width = kv_count * HD
    k_cols = lax.dynamic_slice_in_dim(k_weight, kv_first * HD, kv_width, 1)
    v_cols = lax.dynamic_slice_in_dim(v_weight, kv_first * HD, kv_width, 1)
    k_gain_part = lax.dynamic_slice_in_dim(k_gain, kv_first * HD, kv_width, 0)
    seq_len = hidden_in.shape[0] * tensor_size
    all_tokens = lax.all_gather(hidden_in, "tensor", axis=0, tiled=True)
    weight_pieces = (
        lax.all_gather(q_weight, "dp", axis=0, tiled=True),
        lax.all_gather(k_cols, "dp", axis=0, tiled=True),
        lax.all_gather(v_cols, "dp", axis=0, tiled=True),
    )
    queries, key_rows, value_rows = tuple(
        (
            jnp.dot(all_tokens, weight_piece, preferred_element_type=jnp.float32)
            for weight_piece in weight_pieces
        )
    )
    q_local = jnp.sum(queries * queries, axis=1)
    k_local = jnp.sum(key_rows * key_rows, axis=1) * k_share
    q_total = lax.psum(q_local, "tensor")
    k_total = lax.psum(k_local, "tensor")
    q_normed = (queries * lax.rsqrt(q_total / (heads_all * HD) + epsilon)[:, None] * q_gain).astype(
        jnp.bfloat16
    )
    k_normed = (
        key_rows * lax.rsqrt(k_total / (KV_HEADS * HD) + epsilon)[:, None] * k_gain_part
    ).astype(jnp.bfloat16)
    value_cast = value_rows.astype(jnp.bfloat16)
    q_heads = q_normed.reshape(seq_len, heads_dev, HD)
    k_three = k_normed.reshape(seq_len, kv_count, HD)
    v_three = value_cast.reshape(seq_len, kv_count, HD)
    if heads_dev >= group_size:
        k_heads = jnp.repeat(k_three, group_size, axis=1)
        v_heads = jnp.repeat(v_three, group_size, axis=1)
    else:
        k_heads = jnp.broadcast_to(k_three, (seq_len, heads_dev, HD))
        v_heads = jnp.broadcast_to(v_three, (seq_len, heads_dev, HD))
    scores = jnp.einsum(
        "qhd,khd->hqk", q_heads, k_heads, preferred_element_type=jnp.float32
    ) * HD ** (-0.5)
    rows_idx = lax.broadcasted_iota(jnp.int32, (seq_len, seq_len), 0)
    cols_idx = lax.broadcasted_iota(jnp.int32, (seq_len, seq_len), 1)
    scores = jnp.where((cols_idx <= rows_idx)[None], scores, -1e30)
    row_max = jnp.max(scores, axis=-1, keepdims=True)
    expo = jnp.exp(scores - row_max)
    soft_weights = (expo / jnp.sum(expo, axis=-1, keepdims=True)).astype(jnp.bfloat16)
    attended = jnp.einsum("hqk,khd->qhd", soft_weights, v_heads, preferred_element_type=jnp.float32)
    attended = attended.astype(jnp.bfloat16).reshape(seq_len, q_width)
    partial_value = jnp.dot(
        attended,
        lax.all_gather(o_weight, "dp", axis=1, tiled=True),
        preferred_element_type=jnp.float32,
    )
    summed = lax.psum_scatter(
        partial_value.astype(jnp.bfloat16), "tensor", scatter_dimension=0, tiled=True
    ).astype(jnp.float32)
    mean_square = jnp.mean(summed * summed, axis=1, keepdims=True)
    result = hidden_in.astype(jnp.float32) + summed * lax.rsqrt(mean_square + epsilon) * post_gain
    return result.astype(jnp.bfloat16)


def solution(mesh):
    in_specs = (
        P(("dp", "tensor"), None),
        P("dp", "tensor"),
        P("dp", None),
        P("dp", None),
        P("tensor"),
        P(),
        P("tensor", "dp"),
        P(),
    )
    out_specs = P(("dp", "tensor"), None)
    return jax.shard_map(local, mesh=mesh, in_specs=in_specs, out_specs=out_specs, check_vma=False)
```

profile of v0, /device:TPU:0, one launch (start us, length us, event | category | flops | bytes accessed | tf_op | source)
XLA Modules:
  0.0 380.0 jit_solution(17791873678880812045)
XLA Ops:
  6.5 0.0 copy-start
  6.5 0.0 all-gather.12.cloned.1.call-start
  6.5 1.3 copy-done
  7.9 0.8 constant_dynamic-slice_fusion
  8.6 0.0 all-gather.12.cloned.1.call-update
  8.6 0.0 all-gather.8.cloned.1.call-start
  8.7 0.7 all-gather.8.cloned.1.call-update
  9.4 0.0 all-gather.10.cloned.1.call-start
  9.4 0.7 all-gather.10.cloned.1.call-update
  10.1 0.0 all-gather.6.cloned.1.call-start
  10.2 1.7 constant_dynamic-slice_fusion.1
  11.9 0.0 all-gather.6.cloned.1.call-update
  11.9 0.0 all-gather.14.cloned.1.call-start
  12.0 0.5 all-gather.14.cloned.1.call-update
  12.5 0.0 reduce-scatter.2.cloned.1.call-start
  12.6 0.3 iota_compare_fusion
  12.9 0.8 dynamic_slice.11
  13.7 31.8 %all-gather.12.cloned.1.call-done = bf16[5120,256]{1,0:T(8,128)(2,1)} async-done(((bf16[640,256]{1,0:T(8,128)(2,1)}), bf16[5120,256]{1,0:T(8,128)(2,1)}) %all-gather.12.cloned.1.call-update) | async-done | bytes 2621456 | tf_op jit(solution)/shard_map/all_gather | solution.py:30
  45.4 105.9 %all-gather.8.cloned.1.call-done = bf16[1024,5120]{1,0:T(8,128)(2,1)} async-done(((bf16[256,5120]{1,0:T(8,128)(2,1)}), bf16[1024,5120]{1,0:T(8,128)(2,1)}) %all-gather.8.cloned.1.call-update) | async-done | bytes 10485776 | tf_op jit(solution)/shard_map/all_gather | solution.py:27
  151.4 6.5 %multiply_reduce_fusion = (f32[1024]{0:T(1024)S(1)}, f32[256,1024]{1,0:T(8,128)S(1)}) fusion(bf16[5120,256]{1,0:T(8,128)(2,1)} %all-gather.12.cloned.1.call-done, bf16[1024,5120]{1,0:T(8,128)(2,1)} %all-gather.8.cloned.1.call-done), kind=kOutput, calls=%fused_computation.20 | convolution fusion | flops 2684877824 | bytes 14159872 | tf_op jit(solution)/shard_map/dot_general | solution.py:35
  157.9 0.0 copy-start.2
  157.9 28.8 %all-gather.10.cloned.1.call-done = bf16[5120,256]{1,0:T(8,128)(2,1)} async-done(((bf16[640,256]{1,0:T(8,128)(2,1)}), bf16[5120,256]{1,0:T(8,128)(2,1)}) %all-gather.10.cloned.1.call-update) | async-done | bytes 2621456 | tf_op jit(solution)/shard_map/all_gather | solution.py:29
  186.7 8.6 %multiply_reduce_fusion.1 = (f32[1024]{0:T(1024)S(1)}, f32[1024,256]{0,1:T(8,128)}) fusion(bf16[1024,5120]{1,0:T(8,128)(2,1)} %all-gather.8.cloned.1.call-done, bf16[5120,256]{1,0:T(8,128)(2,1)} %all-gather.10.cloned.1.call-done), kind=kOutput, calls=%fused_computation.22 | convolution fusion | flops 2684877824 | bytes 14159872 | tf_op jit(solution)/shard_map/dot_general | solution.py:35
  195.4 10.2 %all-reduce = (f32[1024]{0:T(1024)S(1)}, f32[1024]{0:T(1024)S(1)}) all-reduce(f32[1024]{0:T(1024)S(1)} %get-tuple-element.7, f32[1024]{0:T(1024)S(1)} %get-tuple-element.9), channel_id=1, replica_groups=mesh['dp'=8,'tensor'=4] {'tensor'}, use_global_device_ids=true, to_apply=%region_1.2 | all-reduce | flops 2048 | bytes 16384 | tf_op jit(solution)/shard_map/psum | solution.py:41
  205.5 0.0 copy-done.2
  205.5 2.1 multiply_convert_fusion.1
  207.7 0.9 multiply_convert_fusion
  208.6 7.9 %fusion.15 = (f32[2,1024]{1,0:T(2,128)S(1)}, f32[2,1024,1024]{1,2,0:T(8,128)}) fusion(pred[1024,1024]{0,1:T(8,128)(4,1)S(1)} %iota_compare_fusion, bf16[1024,2,128]{0,2,1:T(8,128)(2,1)} %bitcast.23, bf16[1024,2,128]{0,2,1:T(8,128)(2,1)} %bitcast.24), kind=kOutput, calls=%fused_computation.31 | convolution fusion | flops 545260544 | bytes 10493952 | tf_op jit(solution)/shard_map/sub | solution.py:66
  216.5 4.6 %all-gather.6.cloned.1.call-done = bf16[5120,256]{1,0:T(8,128)(2,1)} async-done(((bf16[640,256]{1,0:T(8,128)(2,1)}), bf16[5120,256]{1,0:T(8,128)(2,1)}) %all-gather.6.cloned.1.call-update) | async-done | bytes 2621456 | tf_op jit(solution)/shard_map/all_gather | solution.py:31
  221.1 0.0 copy-start.3
  221.1 7.8 %convolution_convert_fusion.1 = bf16[256,1024]{1,0:T(8,128)(2,1)S(1)} fusion(bf16[5120,256]{1,0:T(8,128)(2,1)} %all-gather.6.cloned.1.call-done, bf16[1024,5120]{1,0:T(8,128)(2,1)} %all-gather.8.cloned.1.call-done), kind=kOutput, calls=%fused_computation.18 | convolution fusion | flops 2684616704 | bytes 13631488 | tf_op jit(solution)/shard_map/dot_general | solution.py:35
  229.0 0.0 copy-done.3
  229.0 0.7 fusion.10
  229.7 25.5 %all-gather.14.cloned.1.call-done = bf16[256,5120]{1,0:T(8,128)(2,1)} async-done(((bf16[256,640]{1,0:T(8,128)(2,1)}), bf16[256,5120]{1,0:T(8,128)(2,1)}) %all-gather.14.cloned.1.call-update) | async-done | bytes 2621456 | tf_op jit(solution)/shard_map/all_gather | solution.py:72
  255.2 7.3 %convolution_convert_fusion = bf16[1024,5120]{1,0:T(8,128)(2,1)} fusion(bf16[1024,256]{0,1:T(8,128)(2,1)S(1)} %bitcast.25, bf16[256,5120]{1,0:T(8,128)(2,1)} %all-gather.14.cloned.1.call-done), kind=kOutput, calls=%fused_computation.1 | convolution fusion | flops 2689597440 | bytes 13631488 | tf_op jit(solution)/shard_map/dot_general | solution.py:70
  262.5 0.0 copy-start.1
  262.5 0.0 reduce-scatter.2.cloned.1.call-update
  262.5 103.0 %reduce-scatter.2.cloned.1.call-done = bf16[256,5120]{1,0:T(8,128)(2,1)} async-done(((bf16[1024,5120]{1,0:T(8,128)(2,1)}), bf16[256,5120]{1,0:T(8,128)(2,1)}) %reduce-scatter.2.cloned.1.call-update) | async-done | bytes 2621456 | tf_op jit(solution)/shard_map/reduce_scatter | solution.py:75
  365.5 2.3 fusion.2
  367.8 0.0 copy-done.1
  367.8 5.3 %fusion.5 = bf16[256,5120]{1,0:T(8,128)(2,1)} fusion(bf16[256,5120]{1,0:T(8,128)(2,1)} %reduce-scatter.2.cloned.1.call-done, bf16[256,5120]{1,0:T(8,128)(2,1)} %param.8, f32[5120]{0:T(1024)S(1)} %copy-done.1, f32[256]{0:T(256)S(1)} %add_rsqrt_fusion.2), kind=kLoop, calls=%fused_computation.11 | loop fusion | flops 7864320 | bytes 7885824 | tf_op jit(solution)/shard_map/convert_element_type | solution.py:80
  (2 shorter events, 0.0 us)
Async XLA Ops:
  6.5 1.3 copy-start
  6.5 38.9 %all-gather.12.cloned.1.call-start = ((), (), s32[]{:S(2)}) async-start(), calls=%async_computation.4 | async-start | bytes 2949120 | tf_op jit(solution)/shard_map/all_gather | solution.py:30
  8.6 142.7 %all-gather.8.cloned.1.call-start = ((), (), s32[]{:S(2)}) async-start(), calls=%async_computation.2 | async-start | bytes 13107200 | tf_op jit(solution)/shard_map/all_gather | solution.py:27
  9.4 177.3 %all-gather.10.cloned.1.call-start = ((), (), s32[]{:S(2)}) async-start(), calls=%async_computation.3 | async-start | bytes 2949120 | tf_op jit(solution)/shard_map/all_gather | solution.py:29
  10.1 211.0 %all-gather.6.cloned.1.call-start = ((), (), s32[]{:S(2)}) async-start(), calls=%async_computation.1 | async-start | bytes 2949120 | tf_op jit(solution)/shard_map/all_gather | solution.py:31
  11.9 243.3 %all-gather.14.cloned.1.call-start = ((), (), s32[]{:S(2)}) async-start(), calls=%async_computation.5 | async-start | bytes 2949120 | tf_op jit(solution)/shard_map/all_gather | solution.py:72
  12.5 352.9 %reduce-scatter.2.cloned.1.call-start = ((), (), s32[]{:S(2)}) async-start(), calls=%async_computation.6 | async-start | bytes 13107200 | tf_op jit(solution)/shard_map/reduce_scatter | solution.py:75
  157.9 47.6 %copy-start.2 = (f32[256]{0:T(256)S(1)}, f32[256]{0:T(256)}, u32[]{:S(2)}) copy-start(f32[256]{0:T(256)} %param.12) | copy-start | bytes 3076
  221.1 7.9 %copy-start.3 = (f32[2,1024,1024]{1,2,0:T(8,128)S(1)}, f32[2,1024,1024]{1,2,0:T(8,128)}, u32[]{:S(2)}) copy-start(f32[2,1024,1024]{1,2,0:T(8,128)} %get-tuple-element.12) | copy-start | bytes 25165828
  262.5 105.3 %copy-start.1 = (f32[5120]{0:T(1024)S(1)}, f32[5120]{0:T(1024)}, u32[]{:S(2)}) copy-start(f32[5120]{0:T(1024)} %param.15) | copy-start | bytes 61444
Sparse Core Ops, SparseCore 0:
  9.0 36.4 all-gather.11
  47.3 104.0 all-gather.7
  153.0 33.6 all-gather.9
  188.2 32.8 all-gather.5
  222.6 32.6 all-gather.13
  262.6 102.7 reduce-scatter.1
where the time goes:
time: 380 us
  waiting for transfers between devices  302 us (79%)
  matrix products  38.9 us (10%)
  between operations  13.6 us (4%)
  other arithmetic  11 us (3%)
  blocking collectives  10.2 us (3%)
  local copies, waits for them, and re-layouts  4.6 us (1%)
    all_gather x1, waiting for transfers between devices, local(): all_tokens = lax.all_gather(hidden_in, 'tensor', axis=0, tiled=True)  106 us
    reduce_scatter x1, waiting for transfers between devices, local(): lax.psum_scatter(partial_value.astype(jnp.bfloat16), 'tensor', scatter_di...  103 us
    all_gather x1, waiting for transfers between devices, local(): lax.all_gather(k_cols, 'dp', axis=0, tiled=True)  31.8 us
    all_gather x1, waiting for transfers between devices, local(): lax.all_gather(q_weight, 'dp', axis=0, tiled=True)  28.8 us
    all_gather x1, waiting for transfers between devices, local(): lax.all_gather(o_weight, 'dp', axis=1, tiled=True)  25.5 us
    dot_general x3, matrix products, local(): jnp.dot(all_tokens, weight_piece, preferred_element_type=jnp.float32)  23 us
    psum x1, blocking collectives, local(): q_total = lax.psum(q_local, 'tensor')  10.2 us
    sub x1, matrix products, local(): expo = jnp.exp(scores - row_max)  7.95 us
  transfers between devices with their start and end apart: 6, of which 6 were waited for; matrix products, arithmetic and copies ran while one was open for 10% of the time, Pallas kernels for 0%

commit v1 on v0

v1 whole, which is shorter than its diff:
```python
import functools

import jax
import jax.numpy as jnp
from jax import lax
from jax.experimental import pallas as pl
from jax.experimental.pallas import tpu as pltpu
from jax.sharding import PartitionSpec as P

HD = 128
KV_HEADS = 8
CORES = 2
MESH = pl.DeviceIdType.MESH

epsilon = 1e-06


def plane_of(tensor_size):
    ny = max(n for n in range(1, tensor_size + 1) if tensor_size % n == 0 and n * n <= tensor_size)
    return ny, tensor_size // ny


class Copies:
    def __init__(self, send_sem, recv_sem):
        self.send_sem, self.recv_sem, self.count, self.sent = send_sem, recv_sem, 0, []

    def slot(self):
        self.count += 1
        return self.count - 1

    def make(self, slot, src, dst, device):
        return pltpu.make_async_remote_copy(
            src_ref=src,
            dst_ref=dst,
            send_sem=self.send_sem.at[slot],
            recv_sem=self.recv_sem.at[slot],
            device_id=device,
            device_id_type=MESH,
        )

    def send(self, slot, src, dst, device, when=None):
        copy = self.make(slot, src, dst, device)
        self.sent.append((copy, when))
        run(when, copy.start)

    def receive(self, slot, dst, device, when=None):
        run(when, self.make(slot, dst, dst, device).wait_recv)

    def finish(self):
        for copy, when in self.sent:
            run(when, copy.wait_send)


def run(when, action):
    if when is None:
        action()
    else:
        pl.when(when)(action)


def gather_kernel(
    plan, hid, qw, kw, vw, ow, tok, wts, full, hid_v, w_v, o_v, local_sem, send_sem, recv_sem
):
    ny, nx, nz, q_width, kv_width, kv_step, group = plan
    t, d = lax.axis_index("tensor"), lax.axis_index("dp")
    tx, ty = lax.rem(t, nx), lax.div(t, nx)
    c, z = lax.rem(d, CORES), lax.div(d, CORES)
    rows, depth = hid.shape[0], qw.shape[0]
    o_rows, o_cols = ow.shape
    copies = Copies(send_sem, recv_sem)

    def at_x(j):
        return {"tensor": ty * nx + lax.rem(tx + j, nx), "dp": d}

    def at_y(j):
        return {"tensor": lax.rem(ty + j, ny) * nx + tx, "dp": d}

    up = {"tensor": t, "dp": jnp.minimum(d + CORES, nz * CORES - 1)}
    down = {"tensor": t, "dp": jnp.maximum(d - CORES, 0)}
    partner = {"tensor": t, "dp": z * CORES + 1 - c}
    has_up, has_down = z + 1 < nz, z > 0

    kv_first = pl.multiple_of(lax.div(t * kv_step, group) * HD, HD)
    loads = [
        pltpu.make_async_copy(qw, w_v.at[:, pl.ds(0, q_width)], local_sem.at[0]),
        pltpu.make_async_copy(
            kw.at[:, pl.ds(kv_first, kv_width)], w_v.at[:, pl.ds(q_width, kv_width)], local_sem.at[1]
        ),
        pltpu.make_async_copy(
            vw.at[:, pl.ds(kv_first, kv_width)],
            w_v.at[:, pl.ds(q_width + kv_width, kv_width)],
            local_sem.at[2],
        ),
        pltpu.make_async_copy(hid, hid_v, local_sem.at[3]),
        pltpu.make_async_copy(ow, o_v, local_sem.at[4]),
    ]
    for load in loads:
        load.start()

    barrier = pltpu.get_barrier_semaphore()

    def greet(device):
        pl.semaphore_signal(barrier, inc=1, device_id=device, device_id_type=MESH)

    for j in range(1, nx):
        greet(at_x(j))
    for j in range(1, ny):
        greet(at_y(j))
    greet(partner)
    run(has_up, lambda: greet(up))
    run(has_down, lambda: greet(down))
    pl.semaphore_wait(
        barrier, nx + ny - 1 + has_up.astype(jnp.int32) + has_down.astype(jnp.int32)
    )

    def w_at(dp):
        return wts.at[pl.ds(pl.multiple_of(dp * depth, 8), depth), :]

    def o_at(tensor, dp, part=None):
        size = o_rows if part is None else o_rows // 2
        start = tensor * o_rows + (0 if part is None else part * size)
        return full.at[dp, pl.ds(pl.multiple_of(start, 8), size), :]

    def tok_at(tensor, part):
        size = rows // 2
        return tok.at[pl.ds(pl.multiple_of(tensor * rows + part * size, 8), size), :]

    for load in loads:
        load.wait()
    line = {}
    for name in ("w", "o"):
        for way in ("up", "down"):
            for s in range(1, nz):
                line[name, way, s] = copies.slot()
    links = (("up", up, has_up, 1), ("down", down, has_down, -1))
    for way, device, has, sign in links:
        copies.send(line["w", way, 1], w_v, w_at(d), device, has)

    class Plane:
        def __init__(self, at):
            self.at = at
            self.first = {(p, j): copies.slot() for p in (0, 1) for j in range(1, (nx, ny)[p])}
            self.second = {
                (p, i, j): copies.slot()
                for p in (0, 1)
                for i in range((nx, ny)[p])
                for j in range(1, (ny, nx)[p])
            }

        def source(self, part, i):
            if part == 0:
                return ty * nx + lax.rem(tx - i + nx, nx)
            return lax.rem(ty - i + ny, ny) * nx + tx

        def start(self, src):
            for p in (0, 1):
                for j in range(1, (nx, ny)[p]):
                    copies.send(self.first[p, j], src(p), self.at(t, p), (at_x, at_y)[p](j))
            for p in (0, 1):
                self.cross(p, 0, src(p))

        def cross(self, p, i, src):
            for j in range(1, (ny, nx)[p]):
                copies.send(
                    self.second[p, i, j], src, self.at(self.source(p, i), p), (at_y, at_x)[p](j)
                )

        def forward(self):
            for p in (0, 1):
                for i in range(1, (nx, ny)[p]):
                    block = self.at(self.source(p, i), p)
                    copies.receive(self.first[p, i], block, (at_x, at_y)[p](i))
                    self.cross(p, i, block)

        def finish(self):
            for p in (0, 1):
                for i in range((nx, ny)[p]):
                    for j in range(1, (ny, nx)[p]):
                        if p == 0:
                            came = lax.rem(ty - j + ny, ny) * nx + lax.rem(tx - i + nx, nx)
                        else:
                            came = lax.rem(ty - i + ny, ny) * nx + lax.rem(tx - j + nx, nx)
                        copies.receive(self.second[p, i, j], self.at(came, p), (at_y, at_x)[p](j))

    tokens = Plane(tok_at)
    half = rows // 2
    tokens.start(lambda p: hid_v.at[pl.ds(p * half, half), :])
    for way, device, has, sign in links:
        copies.send(line["o", way, 1], o_v, o_at(t, d), device, has)
    to_partner = {}
    for s in range(1 - nz, nz):
        to_partner["w", s] = copies.slot()
        to_partner["o", s] = copies.slot()
    copies.send(to_partner["w", 0], w_v, w_at(d), partner)
    stores = [
        pltpu.make_async_copy(w_v, w_at(d), local_sem.at[0]),
        pltpu.make_async_copy(hid_v, tok.at[pl.ds(pl.multiple_of(t * rows, 8), rows), :], local_sem.at[3]),
        pltpu.make_async_copy(o_v, o_at(t, d), local_sem.at[4]),
    ]
    for store in stores:
        store.start()

    def pass_on(name, place, s):
        for way, device, has, sign in links:
            here = (z >= s) if way == "up" else (z + s < nz)
            dp = jnp.clip(d - sign * s * CORES, 0, nz * CORES - 1)
            block = place(dp)
            copies.receive(line[name, way, s], block, device, here)
            if s + 1 < nz:
                copies.send(line[name, way, s + 1], block, block, device, here & has)
            if name == "w":
                copies.send(to_partner["w", sign * s], block, block, partner, here)

    def o_place(dp):
        return o_at(t, dp)

    planes = []

    def spread(step):
        dp = lax.rem(z + step, nz) * CORES + c
        plane = Plane(lambda tensor, p: o_at(tensor, dp, p))
        if step == 0:
            oh = o_rows // 2
            plane.start(lambda p: o_v.at[pl.ds(p * oh, oh), :])
        else:
            plane.start(lambda p: o_at(t, dp, p))
        planes.append((plane, dp))

    pass_on("w", w_at, 1)
    tokens.forward()
    spread(0)
    pass_on("o", o_place, 1)
    for s in range(2, nz):
        pass_on("w", w_at, s)
        pass_on("o", o_place, s)
    for store in stores:
        store.wait()
    for step in range(1, nz):
        spread(step)
    for plane, dp in planes:
        plane.forward()
    tokens.finish()
    column_slots = [copies.slot() for _ in planes]
    for slot, (plane, dp) in zip(column_slots, planes):
        plane.finish()
        column = full.at[dp]
        copies.send(slot, column, column, partner)

    copies.receive(to_partner["w", 0], w_at(z * CORES + 1 - c), partner)
    for s in range(1, nz):
        for way, device, has, sign in links:
            here = (z >= s) if way == "up" else (z + s < nz)
            dp = jnp.clip(z - sign * s, 0, nz - 1) * CORES + 1 - c
            copies.receive(to_partner["w", sign * s], w_at(dp), partner, here)
    for step, slot in enumerate(column_slots):
        dp = lax.rem(z + step, nz) * CORES + 1 - c
        column = full.at[dp]
        copies.receive(slot, column, partner)
    copies.finish()


def attend_kernel(
    plan, qkv, q_gain, k_gain, out, sums, q_bf, k_bf, v_bf, att, local_sem, send_sem, recv_sem
):
    tensor_size, heads_dev, kv_count, heads_all, k_share = plan
    t, d = lax.axis_index("tensor"), lax.axis_index("dp")
    q_width, kv_width = heads_dev * HD, kv_count * HD
    seq_len = qkv.shape[0]
    rows = seq_len // tensor_size
    copies = Copies(send_sem, recv_sem)

    def at(j):
        return {"tensor": lax.rem(t + j, tensor_size), "dp": d}

    barrier = pltpu.get_barrier_semaphore()
    for j in range(1, tensor_size):
        pl.semaphore_signal(barrier, inc=1, device_id=at(j), device_id_type=MESH)

    queries = qkv[:, :q_width]
    key_rows = qkv[:, q_width : q_width + kv_width]

    def row_sums(block):
        ones = jnp.ones((8, block.shape[1]), jnp.float32)
        return lax.dot_general(
            ones,
            block * block,
            (((1,), (1,)), ((), ())),
            precision=lax.Precision.HIGHEST,
            preferred_element_type=jnp.float32,
        )

    upper = lax.broadcasted_iota(jnp.int32, (8, seq_len), 0) < 4
    sums[0] = jnp.where(upper, row_sums(queries), row_sums(key_rows) * k_share)
    pl.semaphore_wait(barrier, tensor_size - 1)
    slots = [copies.slot() for _ in range(1, tensor_size)]
    for j in range(1, tensor_size):
        copies.send(slots[j - 1], sums.at[0], sums.at[j], at(j))
    v_bf[...] = qkv[:, q_width + kv_width :].astype(jnp.bfloat16)
    for j in range(1, tensor_size):
        copies.receive(slots[j - 1], sums.at[j], at(j))
    total = sums[0]
    for j in range(1, tensor_size):
        total = total + sums[j]

    def as_column(first):
        pick = (lax.broadcasted_iota(jnp.int32, (8, HD), 0) == first).astype(jnp.float32)
        return lax.dot_general(
            total,
            pick,
            (((0,), (0,)), ((), ())),
            precision=lax.Precision.HIGHEST,
            preferred_element_type=jnp.float32,
        )

    q_scale = lax.rsqrt(as_column(0) / (heads_all * HD) + epsilon)
    k_scale = lax.rsqrt(as_column(4) / (KV_HEADS * HD) + epsilon)
    for h in range(heads_dev):
        cols = slice(h * HD, (h + 1) * HD)
        q_bf[:, cols] = (qkv[:, cols] * q_scale * q_gain[:, cols]).astype(jnp.bfloat16)
    for g in range(kv_count):
        cols = slice(g * HD, (g + 1) * HD)
        source = slice(q_width + g * HD, q_width + (g + 1) * HD)
        k_bf[:, cols] = (qkv[:, source] * k_scale * k_gain[:, cols]).astype(jnp.bfloat16)

    def columns(tensor):
        return out.at[:, pl.ds(pl.multiple_of(tensor * q_width, HD), q_width)]

    back = [copies.slot() for _ in range(tensor_size)]
    for i in range(tensor_size):
        block, seen = slice(i * rows, (i + 1) * rows), (i + 1) * rows
        rows_idx = lax.broadcasted_iota(jnp.int32, (rows, seen), 0) + i * rows
        cols_idx = lax.broadcasted_iota(jnp.int32, (rows, seen), 1)
        for h in range(heads_dev):
            g = h * kv_count // heads_dev
            cols, kv_cols = slice(h * HD, (h + 1) * HD), slice(g * HD, (g + 1) * HD)
            scores = lax.dot_general(
                q_bf[block, cols],
                k_bf[:seen, kv_cols],
                (((1,), (1,)), ((), ())),
                preferred_element_type=jnp.float32,
            ) * HD ** (-0.5)
            scores = jnp.where(cols_idx <= rows_idx, scores, -1e30)
            expo = jnp.exp(scores - jnp.max(scores, axis=1, keepdims=True))
            weights = (expo * (1.0 / jnp.sum(expo, axis=1, keepdims=True))).astype(jnp.bfloat16)
            att[block, cols] = jnp.dot(
                weights, v_bf[:seen, kv_cols], preferred_element_type=jnp.float32
            ).astype(jnp.bfloat16)
        own = att.at[pl.ds(i * rows, rows), :]
        j = lax.rem(i - t + tensor_size, tensor_size)
        copy = pltpu.make_async_remote_copy(
            src_ref=own,
            dst_ref=columns(t),
            send_sem=send_sem.at[back[i]],
            recv_sem=recv_sem.at[back[0] + j],
            device_id={"tensor": i, "dp": d},
            device_id_type=MESH,
        )
        copies.sent.append((copy, t != i))
        pl.when(t != i)(copy.start)
    mine = pltpu.make_async_copy(
        att.at[pl.ds(pl.multiple_of(t * rows, 8), rows), :], columns(t), local_sem.at[0]
    )
    mine.start()
    mine.wait()
    for j in range(1, tensor_size):
        copies.receive(back[j], columns(lax.rem(t - j + tensor_size, tensor_size)), at(j))
    copies.finish()


def project_kernel(att, weight, hid, gain, out, projected, squares):
    n = pl.program_id(0)
    blocks, _, cols = projected.shape
    block = jnp.dot(att[...], weight[0], preferred_element_type=jnp.float32)
    projected[n] = block
    here = jnp.sum(block * block, axis=1, keepdims=True)

    @pl.when(n == 0)
    def _():
        squares[...] = here

    @pl.when(n > 0)
    def _():
        squares[...] += here

    @pl.when(n == blocks - 1)
    def _():
        scale = lax.rsqrt(squares[...] / (blocks * cols) + epsilon)
        for b in range(blocks):
            part = slice(b * cols, (b + 1) * cols)
            out[:, part] = (
                hid[:, part].astype(jnp.float32) + projected[b] * scale * gain[:, part]
            ).astype(out.dtype)


def local(hidden_in, q_weight, k_weight, v_weight, q_gain, k_gain, o_weight, post_gain):
    tensor_size, dp_size = lax.axis_size("tensor"), lax.axis_size("dp")
    heads_dev = q_weight.shape[1] // HD
    heads_all = heads_dev * tensor_size
    group_size = heads_all // KV_HEADS
    kv_count = max(1, heads_dev // group_size)
    kv_first = lax.axis_index("tensor") * heads_dev // group_size
    k_share = min(1.0, heads_dev / group_size)
    q_width, kv_width = heads_dev * HD, kv_count * HD
    width = q_width + 2 * kv_width
    rows, model = hidden_in.shape
    depth = q_weight.shape[0]
    o_rows, o_cols = o_weight.shape
    seq_len = rows * tensor_size
    ny, nx = plane_of(tensor_size)
    nz = dp_size // CORES
    any_space = pl.BlockSpec(memory_space=pl.ANY)
    vmem = pl.BlockSpec(memory_space=pltpu.VMEM)
    bf16 = jnp.bfloat16

    per_plane = (nx - 1) + (ny - 1) + nx * (ny - 1) + ny * (nx - 1)
    slots = 4 * (nz - 1) + (nz + 1) * per_plane + 2 * (2 * nz - 1) + nz
    tokens, weights, o_full = pl.pallas_call(
        functools.partial(
            gather_kernel, (ny, nx, nz, q_width, kv_width, heads_dev, group_size)
        ),
        out_shape=(
            jax.ShapeDtypeStruct((seq_len, model), bf16),
            jax.ShapeDtypeStruct((depth * dp_size, width), bf16),
            jax.ShapeDtypeStruct((dp_size, o_rows * tensor_size, o_cols), bf16),
        ),
        in_specs=[any_space] * 5,
        out_specs=(any_space,) * 3,
        scratch_shapes=[
            pltpu.VMEM((rows, model), bf16),
            pltpu.VMEM((depth, width), bf16),
            pltpu.VMEM((o_rows, o_cols), bf16),
            pltpu.SemaphoreType.DMA((5,)),
            pltpu.SemaphoreType.DMA((slots,)),
            pltpu.SemaphoreType.DMA((slots,)),
        ],
        compiler_params=pltpu.CompilerParams(collective_id=0, has_side_effects=True),
        name="gather",
    )(hidden_in, q_weight, k_weight, v_weight, o_weight)

    qkv = jnp.dot(tokens, weights, preferred_element_type=jnp.float32)
    k_gain_part = lax.dynamic_slice_in_dim(k_gain, kv_first * HD, kv_width, 0)
    attended = pl.pallas_call(
        functools.partial(attend_kernel, (tensor_size, heads_dev, kv_count, heads_all, k_share)),
        out_shape=jax.ShapeDtypeStruct((rows, q_width * tensor_size), bf16),
        in_specs=[vmem] * 3,
        out_specs=any_space,
        scratch_shapes=[
            pltpu.VMEM((tensor_size, 8, seq_len), jnp.float32),
            pltpu.VMEM((seq_len, q_width), bf16),
            pltpu.VMEM((seq_len, kv_width), bf16),
            pltpu.VMEM((seq_len, kv_width), bf16),
            pltpu.VMEM((seq_len, q_width), bf16),
            pltpu.SemaphoreType.DMA((1,)),
            pltpu.SemaphoreType.DMA((2 * tensor_size,)),
            pltpu.SemaphoreType.DMA((2 * tensor_size,)),
        ],
        compiler_params=pltpu.CompilerParams(collective_id=1, has_side_effects=True),
        name="attend",
    )(qkv, q_gain[None], k_gain_part[None])

    return pl.pallas_call(
        project_kernel,
        out_shape=jax.ShapeDtypeStruct((rows, model), bf16),
        grid=(dp_size,),
        in_specs=[
            pl.BlockSpec(attended.shape, lambda n: (0, 0)),
            pl.BlockSpec((1,) + o_full.shape[1:], lambda n: (n, 0, 0)),
            pl.BlockSpec((rows, model), lambda n: (0, 0)),
            pl.BlockSpec((1, model), lambda n: (0, 0)),
        ],
        out_specs=pl.BlockSpec((rows, model), lambda n: (0, 0)),
        scratch_shapes=[
            pltpu.VMEM((dp_size, rows, o_cols), jnp.float32),
            pltpu.VMEM((rows, 1), jnp.float32),
        ],
        name="project",
    )(attended, o_full, hidden_in, post_gain[None])


def solution(mesh):
    in_specs = (
        P(("dp", "tensor"), None),
        P("dp", "tensor"),
        P("dp", None),
        P("dp", None),
        P("tensor"),
        P(),
        P("tensor", "dp"),
        P(),
    )
    out_specs = P(("dp", "tensor"), None)
    return jax.shard_map(local, mesh=mesh, in_specs=in_specs, out_specs=out_specs, check_vma=False)
```

time: 380 us -> 184 us (0.48)
  waiting for transfers between devices: 302 us -> 0 us
  Pallas kernels: 0 us -> 167 us
  matrix products: 38.9 us -> 14.4 us
  between operations: 13.6 us -> 0.02 us
  other arithmetic: 11 us -> 0 us
  blocking collectives: 10.2 us -> 0 us
    all_gather x5 -> x0, waiting for transfers between devices: 197 us -> none  [the longest x1 106 us: local(): all_tokens = lax.all_gather(hidden_in, 'tensor', axis=0, tiled=True)]
    pallas_call x0 -> x3, Pallas kernels: none -> 167 us  [the longest x1 136 us: local(): pl.pallas_call(functools.partial(gather_kernel, (ny, nx, nz, q_width, kv_...]
    reduce_scatter x1 -> x0, waiting for transfers between devices: 103 us -> none  [local(): lax.psum_scatter(partial_value.astype(jnp.bfloat16), 'tensor', scatter_di...]
    dot_general x5 -> x1, matrix products: 31 us -> 14.4 us  [local(): qkv = jnp.dot(tokens, weights, preferred_element_type=jnp.float32)]
    psum x1 -> x0, blocking collectives: 10.2 us -> none  [local(): q_total = lax.psum(q_local, 'tensor')]
    convert_element_type x3 -> x0, other arithmetic: 8.38 us -> none  [the longest x1 5.33 us: local(): return result.astype(jnp.bfloat16)]
    sub x1 -> x0, matrix products: 7.95 us -> none  [local(): expo = jnp.exp(scores - row_max)]
  transfers between devices with their start and end apart: 6 -> 0, of which waited for: 6 -> 0; matrix products, arithmetic and copies ran while one was open for 10% -> 0% of each run, Pallas kernels for 0% -> 0%
where the time goes in v1:
time: 184 us; the launch traced here: 183 us
  Pallas kernels  167 us (91%)
  matrix products  14.4 us (8%)
    pallas_call x1, Pallas kernels, local(): pl.pallas_call(functools.partial(gather_kernel, (ny, nx, nz, q_width, kv_...  136 us
    pallas_call x1, Pallas kernels, local(): pl.pallas_call(functools.partial(attend_kernel, (tensor_size, heads_dev,...  18.1 us
    dot_general x1, matrix products, local(): qkv = jnp.dot(tokens, weights, preferred_element_type=jnp.float32)  14.4 us
    pallas_call x1, Pallas kernels, local(): pl.pallas_call(project_kernel, out_shape=jax.ShapeDtypeStruct((rows, mode...  12.9 us

profile of v1, /device:TPU:0, one launch (start us, length us, event | category | flops | bytes accessed | tf_op | source)
XLA Modules:
  0.0 183.1 jit_solution(808883309894297511)
XLA Ops:
  0.0 136.4 %gather.1 = (bf16[1024,5120]{1,0:T(8,128)(2,1)}, bf16[5120,768]{1,0:T(8,128)(2,1)}, bf16[8,1024,640]{2,1,0:T(8,128)(2,1)}) custom-call(bf16[256,5120]{1,0:T(8,128)(2,1)} %hid.3, bf16[640,256]{1,0:T(8,128)(2,1)} %qw.1, bf16[640,1024]{1,0:T(8,128)(2,1)} %kw.1, bf16[640,1024]{1,0:T(8,128)(2,1)} %vw.1, bf16[256,640]{1,0:T(8,128)(2,1)} %ow.1), custom_call_target="tpu_custom_call" | custom-call | tf_op jit(solution)/shard_map/gather/pallas_call | solution.py:417
  136.4 14.4 %fusion.qkv = f32[1024,768]{1,0:T(8,128)} fusion(bf16[1024,5120]{1,0:T(8,128)(2,1)} %get-tuple-element.8, bf16[5120,768]{1,0:T(8,128)(2,1)} %get-tuple-element.9), kind=kOutput, calls=%fused_computation | convolution fusion | flops 8053063680 | bytes 21495808 | tf_op jit(solution)/shard_map/dot_general | solution.py:440
  150.8 1.3 dynamic_slice.3
  152.1 18.1 %attend.1.att = bf16[256,1024]{1,0:T(8,128)(2,1)} custom-call(f32[1024,768]{1,0:T(8,128)} %fusion.qkv, f32[1,256]{1,0:T(1,128)} %bitcast.7, f32[1,256]{1,0:T(1,128)} %bitcast.6), custom_call_target="tpu_custom_call" | custom-call | tf_op jit(solution)/shard_map/attend/pallas_call | solution.py:442
  170.2 12.9 %project.1 = bf16[256,5120]{1,0:T(8,128)(2,1)} custom-call(bf16[256,1024]{1,0:T(8,128)(2,1)} %attend.1.att, bf16[8,1024,640]{2,1,0:T(8,128)(2,1)} %get-tuple-element.10.weight, bf16[256,5120]{1,0:T(8,128)(2,1)} %hid.3, f32[1,5120]{1,0:T(1,128)} %bitcast.5), custom_call_target="tpu_custom_call" | custom-call | tf_op jit(solution)/shard_map/project/pallas_call | solution.py:461

commit v2 on v1

--- a/solution.py
+++ b/solution.py
@@ -58,10 +58,33 @@
         pl.when(when)(action)
 
 
-def gather_kernel(
-    plan, hid, qw, kw, vw, ow, tok, wts, full, hid_v, w_v, o_v, local_sem, send_sem, recv_sem
+def layer_kernel(
+    plan,
+    hid,
+    qw,
+    kw,
+    vw,
+    ow,
+    q_gain,
+    k_gain,
+    full,
+    out,
+    tok,
+    wts,
+    o_v,
+    qkv,
+    sums,
+    q_bf,
+    k_bf,
+    v_bf,
+    att,
+    local_sem,
+    send_sem,
+    recv_sem,
 ):
-    ny, nx, nz, q_width, kv_width, kv_step, group = plan
+    ny, nx, nz, heads_dev, kv_count, group, k_share = plan
+    q_width, kv_width = heads_dev * HD, kv_count * HD
+    tensor_size = ny * nx
     t, d = lax.axis_index("tensor"), lax.axis_index("dp")
     tx, ty = lax.rem(t, nx), lax.div(t, nx)
     c, z = lax.rem(d, CORES), lax.div(d, CORES)
@@ -80,18 +103,23 @@
     partner = {"tensor": t, "dp": z * CORES + 1 - c}
     has_up, has_down = z + 1 < nz, z > 0
 
-    kv_first = pl.multiple_of(lax.div(t * kv_step, group) * HD, HD)
+    kv_first = pl.multiple_of(lax.div(t * heads_dev, group) * HD, HD)
+    w_rows = pl.ds(pl.multiple_of(d * depth, 8), depth)
     loads = [
-        pltpu.make_async_copy(qw, w_v.at[:, pl.ds(0, q_width)], local_sem.at[0]),
+        pltpu.make_async_copy(qw, wts.at[w_rows, pl.ds(0, q_width)], local_sem.at[0]),
         pltpu.make_async_copy(
-            kw.at[:, pl.ds(kv_first, kv_width)], w_v.at[:, pl.ds(q_width, kv_width)], local_sem.at[1]
+            kw.at[:, pl.ds(kv_first, kv_width)],
+            wts.at[w_rows, pl.ds(q_width, kv_width)],
+            local_sem.at[1],
         ),
         pltpu.make_async_copy(
             vw.at[:, pl.ds(kv_first, kv_width)],
-            w_v.at[:, pl.ds(q_width + kv_width, kv_width)],
+            wts.at[w_rows, pl.ds(q_width + kv_width, kv_width)],
             local_sem.at[2],
         ),
-        pltpu.make_async_copy(hid, hid_v, local_sem.at[3]),
+        pltpu.make_async_copy(
+            hid, tok.at[pl.ds(pl.multiple_of(t * rows, 8), rows), :], local_sem.at[3]
+        ),
         pltpu.make_async_copy(ow, o_v, local_sem.at[4]),
     ]
     for load in loads:
@@ -102,15 +130,13 @@
     def greet(device):
         pl.semaphore_signal(barrier, inc=1, device_id=device, device_id_type=MESH)
 
-    for j in range(1, nx):
-        greet(at_x(j))
-    for j in range(1, ny):
-        greet(at_y(j))
+    for j in range(1, tensor_size):
+        greet({"tensor": lax.rem(t + j, tensor_size), "dp": d})
     greet(partner)
     run(has_up, lambda: greet(up))
     run(has_down, lambda: greet(down))
     pl.semaphore_wait(
-        barrier, nx + ny - 1 + has_up.astype(jnp.int32) + has_down.astype(jnp.int32)
+        barrier, tensor_size + has_up.astype(jnp.int32) + has_down.astype(jnp.int32)
     )
 
     def w_at(dp):
@@ -134,7 +160,7 @@
                 line[name, way, s] = copies.slot()
     links = (("up", up, has_up, 1), ("down", down, has_down, -1))
     for way, device, has, sign in links:
-        copies.send(line["w", way, 1], w_v, w_at(d), device, has)
+        copies.send(line["w", way, 1], w_at(d), w_at(d), device, has)
 
     class Plane:
         def __init__(self, at):
@@ -183,22 +209,16 @@
                         copies.receive(self.second[p, i, j], self.at(came, p), (at_y, at_x)[p](j))
 
     tokens = Plane(tok_at)
-    half = rows // 2
-    tokens.start(lambda p: hid_v.at[pl.ds(p * half, half), :])
+    tokens.start(lambda p: tok_at(t, p))
     for way, device, has, sign in links:
         copies.send(line["o", way, 1], o_v, o_at(t, d), device, has)
     to_partner = {}
     for s in range(1 - nz, nz):
         to_partner["w", s] = copies.slot()
         to_partner["o", s] = copies.slot()
-    copies.send(to_partner["w", 0], w_v, w_at(d), partner)
-    stores = [
-        pltpu.make_async_copy(w_v, w_at(d), local_sem.at[0]),
-        pltpu.make_async_copy(hid_v, tok.at[pl.ds(pl.multiple_of(t * rows, 8), rows), :], local_sem.at[3]),
-        pltpu.make_async_copy(o_v, o_at(t, d), local_sem.at[4]),
-    ]
-    for store in stores:
-        store.start()
+    copies.send(to_partner["w", 0], w_at(d), w_at(d), partner)
+    store = pltpu.make_async_copy(o_v, o_at(t, d), local_sem.at[4])
+    store.start()
 
     def pass_on(name, place, s):
         for way, device, has, sign in links:
@@ -233,48 +253,78 @@
     for s in range(2, nz):
         pass_on("w", w_at, s)
         pass_on("o", o_place, s)
-    for store in stores:
-        store.wait()
+    store.wait()
     for step in range(1, nz):
         spread(step)
-    for plane, dp in planes:
-        plane.forward()
-    tokens.finish()
-    column_slots = [copies.slot() for _ in planes]
-    for slot, (plane, dp) in zip(column_slots, planes):
-        plane.finish()
-        column = full.at[dp]
-        copies.send(slot, column, column, partner)
-
     copies.receive(to_partner["w", 0], w_at(z * CORES + 1 - c), partner)
     for s in range(1, nz):
         for way, device, has, sign in links:
             here = (z >= s) if way == "up" else (z + s < nz)
             dp = jnp.clip(z - sign * s, 0, nz - 1) * CORES + 1 - c
             copies.receive(to_partner["w", sign * s], w_at(dp), partner, here)
+
+    width = wts.shape[1]
+    step_cols = 2 * HD if width % (2 * HD) == 0 else HD
+
+    def multiply(tensor):
+        block = pl.ds(pl.multiple_of(tensor * rows, 8), rows)
+
+        def one(n, carry):
+            cols = pl.ds(pl.multiple_of(n * step_cols, HD), step_cols)
+            qkv[block, cols] = jnp.dot(
+                tok[block, :], wts[:, cols], preferred_element_type=jnp.float32
+            )
+            return carry
+
+        lax.fori_loop(0, width // step_cols, one, 0)
+
+    multiply(t)
+    tokens.finish()
+
+    def others(j, carry):
+        multiply(lax.rem(t + j, tensor_size))
+        return carry
+
+    lax.fori_loop(1, tensor_size, others, 0)
+    for plane, dp in planes:
+        plane.forward()
+    attend(
+        (tensor_size, heads_dev, kv_count, heads_dev * tensor_size, k_share),
+        copies,
+        qkv,
+        q_gain,
+        k_gain,
+        kv_first,
+        out,
+        sums,
+        q_bf,
+        k_bf,
+        v_bf,
+        att,
+        local_sem,
+    )
+    column_slots = [copies.slot() for _ in planes]
+    for slot, (plane, dp) in zip(column_slots, planes):
+        plane.finish()
+        copies.send(slot, full.at[dp], full.at[dp], partner)
     for step, slot in enumerate(column_slots):
         dp = lax.rem(z + step, nz) * CORES + 1 - c
-        column = full.at[dp]
-        copies.receive(slot, column, partner)
+        copies.receive(slot, full.at[dp], partner)
     copies.finish()
 
 
-def attend_kernel(
-    plan, qkv, q_gain, k_gain, out, sums, q_bf, k_bf, v_bf, att, local_sem, send_sem, recv_sem
+def attend(
+    plan, copies, qkv, q_gain, k_gain, kv_first, out, sums, q_bf, k_bf, v_bf, att, local_sem
 ):
     tensor_size, heads_dev, kv_count, heads_all, k_share = plan
     t, d = lax.axis_index("tensor"), lax.axis_index("dp")
     q_width, kv_width = heads_dev * HD, kv_count * HD
     seq_len = qkv.shape[0]
     rows = seq_len // tensor_size
-    copies = Copies(send_sem, recv_sem)
+    send_sem, recv_sem = copies.send_sem, copies.recv_sem
 
     def at(j):
         return {"tensor": lax.rem(t + j, tensor_size), "dp": d}
-
-    barrier = pltpu.get_barrier_semaphore()
-    for j in range(1, tensor_size):
-        pl.semaphore_signal(barrier, inc=1, device_id=at(j), device_id_type=MESH)
 
     queries = qkv[:, :q_width]
     key_rows = qkv[:, q_width : q_width + kv_width]
@@ -291,7 +341,6 @@
 
     upper = lax.broadcasted_iota(jnp.int32, (8, seq_len), 0) < 4
     sums[0] = jnp.where(upper, row_sums(queries), row_sums(key_rows) * k_share)
-    pl.semaphore_wait(barrier, tensor_size - 1)
     slots = [copies.slot() for _ in range(1, tensor_size)]
     for j in range(1, tensor_size):
         copies.send(slots[j - 1], sums.at[0], sums.at[j], at(j))
@@ -319,8 +368,9 @@
         q_bf[:, cols] = (qkv[:, cols] * q_scale * q_gain[:, cols]).astype(jnp.bfloat16)
     for g in range(kv_count):
         cols = slice(g * HD, (g + 1) * HD)
+        gain = k_gain[:, pl.ds(pl.multiple_of(kv_first + g * HD, HD), HD)]
         source = slice(q_width + g * HD, q_width + (g + 1) * HD)
-        k_bf[:, cols] = (qkv[:, source] * k_scale * k_gain[:, cols]).astype(jnp.bfloat16)
+        k_bf[:, cols] = (qkv[:, source] * k_scale * gain).astype(jnp.bfloat16)
 
     def columns(tensor):
         return out.at[:, pl.ds(pl.multiple_of(tensor * q_width, HD), q_width)]
@@ -364,7 +414,6 @@
     mine.wait()
     for j in range(1, tensor_size):
         copies.receive(back[j], columns(lax.rem(t - j + tensor_size, tensor_size)), at(j))
-    copies.finish()
 
 
 def project_kernel(att, weight, hid, gain, out, projected, squares):
@@ -398,7 +447,6 @@
     heads_all = heads_dev * tensor_size
     group_size = heads_all // KV_HEADS
     kv_count = max(1, heads_dev // group_size)
-    kv_first = lax.axis_index("tensor") * heads_dev // group_size
     k_share = min(1.0, heads_dev / group_size)
     q_width, kv_width = heads_dev * HD, kv_count * HD
     width = q_width + 2 * kv_width
@@ -413,50 +461,34 @@
     bf16 = jnp.bfloat16
 
     per_plane = (nx - 1) + (ny - 1) + nx * (ny - 1) + ny * (nx - 1)
-    slots = 4 * (nz - 1) + (nz + 1) * per_plane + 2 * (2 * nz - 1) + nz
-    tokens, weights, o_full = pl.pallas_call(
+    slots = 4 * (nz - 1) + (nz + 1) * per_plane + 2 * (2 * nz - 1) + nz + 2 * tensor_size
+    o_full, attended = pl.pallas_call(
         functools.partial(
-            gather_kernel, (ny, nx, nz, q_width, kv_width, heads_dev, group_size)
+            layer_kernel, (ny, nx, nz, heads_dev, kv_count, group_size, k_share)
         ),
         out_shape=(
-            jax.ShapeDtypeStruct((seq_len, model), bf16),
-            jax.ShapeDtypeStruct((depth * dp_size, width), bf16),
             jax.ShapeDtypeStruct((dp_size, o_rows * tensor_size, o_cols), bf16),
+            jax.ShapeDtypeStruct((rows, q_width * tensor_size), bf16),
         ),
-        in_specs=[any_space] * 5,
-        out_specs=(any_space,) * 3,
+        in_specs=[any_space] * 5 + [vmem] * 2,
+        out_specs=(any_space,) * 2,
         scratch_shapes=[
-            pltpu.VMEM((rows, model), bf16),
-            pltpu.VMEM((depth, width), bf16),
+            pltpu.VMEM((seq_len, model), bf16),
+            pltpu.VMEM((depth * dp_size, width), bf16),
             pltpu.VMEM((o_rows, o_cols), bf16),
+            pltpu.VMEM((seq_len, width), jnp.float32),
+            pltpu.VMEM((tensor_size, 8, seq_len), jnp.float32),
+            pltpu.VMEM((seq_len, q_width), bf16),
+            pltpu.VMEM((seq_len, kv_width), bf16),
+            pltpu.VMEM((seq_len, kv_width), bf16),
+            pltpu.VMEM((seq_len, q_width), bf16),
             pltpu.SemaphoreType.DMA((5,)),
             pltpu.SemaphoreType.DMA((slots,)),
             pltpu.SemaphoreType.DMA((slots,)),
         ],
         compiler_params=pltpu.CompilerParams(collective_id=0, has_side_effects=True),
-        name="gather",
-    )(hidden_in, q_weight, k_weight, v_weight, o_weight)
-
-    qkv = jnp.dot(tokens, weights, preferred_element_type=jnp.float32)
-    k_gain_part = lax.dynamic_slice_in_dim(k_gain, kv_first * HD, kv_width, 0)
-    attended = pl.pallas_call(
-        functools.partial(attend_kernel, (tensor_size, heads_dev, kv_count, heads_all, k_share)),
-        out_shape=jax.ShapeDtypeStruct((rows, q_width * tensor_size), bf16),
-        in_specs=[vmem] * 3,
-        out_specs=any_space,
-        scratch_shapes=[
-            pltpu.VMEM((tensor_size, 8, seq_len), jnp.float32),
-            pltpu.VMEM((seq_len, q_width), bf16),
-            pltpu.VMEM((seq_len, kv_width), bf16),
-            pltpu.VMEM((seq_len, kv_width), bf16),
-            pltpu.VMEM((seq_len, q_width), bf16),
-            pltpu.SemaphoreType.DMA((1,)),
-            pltpu.SemaphoreType.DMA((2 * tensor_size,)),
-            pltpu.SemaphoreType.DMA((2 * tensor_size,)),
-        ],
-        compiler_params=pltpu.CompilerParams(collective_id=1, has_side_effects=True),
-        name="attend",
-    )(qkv, q_gain[None], k_gain_part[None])
+        name="layer",
+    )(hidden_in, q_weight, k_weight, v_weight, o_weight, q_gain[None], k_gain[None])
 
     return pl.pallas_call(
         project_kernel,

time: 184 us -> 168 us (0.913)
  matrix products: 14.4 us -> 0 us
    dot_general x1 -> x0, matrix products: 14.4 us -> none  [local(): qkv = jnp.dot(tokens, weights, preferred_element_type=jnp.float32)]
    pallas_call x2 -> x1, Pallas kernels: 154 us -> 153 us  [local(): pl.pallas_call(functools.partial(layer_kernel, (ny, nx, nz, heads_dev, kv...]
where the time goes in v2:
time: 168 us; the launch traced here: 166 us
  Pallas kernels  166 us (99%)
    pallas_call x1, Pallas kernels, local(): pl.pallas_call(functools.partial(layer_kernel, (ny, nx, nz, heads_dev, kv...  153 us
    pallas_call x1, Pallas kernels, local(): pl.pallas_call(project_kernel, out_shape=jax.ShapeDtypeStruct((rows, mode...  12.9 us

profile of v2, /device:TPU:0, one launch (start us, length us, event | category | flops | bytes accessed | tf_op | source)
XLA Modules:
  0.0 165.7 jit_solution(4797455062975938176)
XLA Ops:
  0.0 152.7 %layer.1 = (bf16[8,1024,640]{2,1,0:T(8,128)(2,1)}, bf16[256,1024]{1,0:T(8,128)(2,1)}) custom-call(bf16[256,5120]{1,0:T(8,128)(2,1)} %hid.3, bf16[640,256]{1,0:T(8,128)(2,1)} %qw.1, bf16[640,1024]{1,0:T(8,128)(2,1)} %kw.1, bf16[640,1024]{1,0:T(8,128)(2,1)} %vw.1, bf16[256,640]{1,0:T(8,128)(2,1)} %ow.1, f32[1,256]{1,0:T(1,128)} %bitcast.5, f32[1,1024]{1,0:T(1,128)} %bitcast.4), custom_call_target="tpu_custom_call" | custom-call | tf_op jit(solution)/shard_map/layer/pallas_call | solution.py:465
  152.7 12.9 %project.1 = bf16[256,5120]{1,0:T(8,128)(2,1)} custom-call(bf16[256,1024]{1,0:T(8,128)(2,1)} %get-tuple-element.7.att, bf16[8,1024,640]{2,1,0:T(8,128)(2,1)} %get-tuple-element.8.weight, bf16[256,5120]{1,0:T(8,128)(2,1)} %hid.3, f32[1,5120]{1,0:T(1,128)} %bitcast.3), custom_call_target="tpu_custom_call" | custom-call | tf_op jit(solution)/shard_map/project/pallas_call | solution.py:493

commit v3 on v2

--- a/solution.py
+++ b/solution.py
@@ -163,8 +163,8 @@
         copies.send(line["w", way, 1], w_at(d), w_at(d), device, has)
 
     class Plane:
-        def __init__(self, at):
-            self.at = at
+        def __init__(self, at, when=None):
+            self.at, self.when = at, when
             self.first = {(p, j): copies.slot() for p in (0, 1) for j in range(1, (nx, ny)[p])}
             self.second = {
                 (p, i, j): copies.slot()
@@ -181,41 +181,46 @@
         def start(self, src):
             for p in (0, 1):
                 for j in range(1, (nx, ny)[p]):
-                    copies.send(self.first[p, j], src(p), self.at(t, p), (at_x, at_y)[p](j))
+                    copies.send(
+                        self.first[p, j], src(p), self.at(t, p), (at_x, at_y)[p](j), self.when
+                    )
             for p in (0, 1):
                 self.cross(p, 0, src(p))
 
         def cross(self, p, i, src):
             for j in range(1, (ny, nx)[p]):
                 copies.send(
-                    self.second[p, i, j], src, self.at(self.source(p, i), p), (at_y, at_x)[p](j)
+                    self.second[p, i, j],
+                    src,
+                    self.at(self.source(p, i), p),
+                    (at_y, at_x)[p](j),
+                    self.when,
                 )
 
         def forward(self):
             for p in (0, 1):
                 for i in range(1, (nx, ny)[p]):
                     block = self.at(self.source(p, i), p)
-                    copies.receive(self.first[p, i], block, (at_x, at_y)[p](i))
+                    copies.receive(self.first[p, i], block, (at_x, at_y)[p](i), self.when)
                     self.cross(p, i, block)
 
-        def finish(self):
+        def finish(self, diagonal=None):
             for p in (0, 1):
                 for i in range((nx, ny)[p]):
                     for j in range(1, (ny, nx)[p]):
-                        if p == 0:
-                            came = lax.rem(ty - j + ny, ny) * nx + lax.rem(tx - i + nx, nx)
-                        else:
-                            came = lax.rem(ty - i + ny, ny) * nx + lax.rem(tx - j + nx, nx)
-                        copies.receive(self.second[p, i, j], self.at(came, p), (at_y, at_x)[p](j))
+                        if diagonal is not None and diagonal != (i > 0):
+                            continue
+                        jx, jy = (i, j) if p == 0 else (j, i)
+                        copies.receive(
+                            self.second[p, i, j], self.at(near(jx, jy), p), (at_y, at_x)[p](j), self.when
+                        )
+
+    def near(jx, jy):
+        return lax.rem(ty - jy + ny, ny) * nx + lax.rem(tx - jx + nx, nx)
 
     tokens = Plane(tok_at)
     tokens.start(lambda p: tok_at(t, p))
-    for way, device, has, sign in links:
-        copies.send(line["o", way, 1], o_v, o_at(t, d), device, has)
-    to_partner = {}
-    for s in range(1 - nz, nz):
-        to_partner["w", s] = copies.slot()
-        to_partner["o", s] = copies.slot()
+    to_partner = {("w", s): copies.slot() for s in range(1 - nz, nz)}
     copies.send(to_partner["w", 0], w_at(d), w_at(d), partner)
     store = pltpu.make_async_copy(o_v, o_at(t, d), local_sem.at[4])
     store.start()
@@ -234,28 +239,29 @@
     def o_place(dp):
         return o_at(t, dp)
 
-    planes = []
-
-    def spread(step):
-        dp = lax.rem(z + step, nz) * CORES + c
-        plane = Plane(lambda tensor, p: o_at(tensor, dp, p))
+    groups = [[] for _ in range(nz)]
+
+    def spread(step, way=None):
+        sign = -1 if way == "down" else 1
+        dp = jnp.clip(d - sign * step * CORES, 0, nz * CORES - 1)
+        when = None if step == 0 else (z >= step) if way == "up" else (z + step < nz)
+        plane = Plane(lambda tensor, p: o_at(tensor, dp, p), when)
+        half = o_rows // 2
         if step == 0:
-            oh = o_rows // 2
-            plane.start(lambda p: o_v.at[pl.ds(p * oh, oh), :])
+            plane.start(lambda p: o_v.at[pl.ds(p * half, half), :])
         else:
             plane.start(lambda p: o_at(t, dp, p))
-        planes.append((plane, dp))
-
-    pass_on("w", w_at, 1)
-    tokens.forward()
-    spread(0)
-    pass_on("o", o_place, 1)
-    for s in range(2, nz):
+        groups[step].append((plane, sign * step))
+
+    for s in range(1, nz):
+        if s == nz - 1:
+            for way, device, has, sign in links:
+                copies.send(line["o", way, 1], o_v, o_at(t, d), device, has)
         pass_on("w", w_at, s)
-        pass_on("o", o_place, s)
+        if s == 1:
+            tokens.forward()
+            spread(0)
     store.wait()
-    for step in range(1, nz):
-        spread(step)
     copies.receive(to_partner["w", 0], w_at(z * CORES + 1 - c), partner)
     for s in range(1, nz):
         for way, device, has, sign in links:
@@ -279,18 +285,30 @@
         lax.fori_loop(0, width // step_cols, one, 0)
 
     multiply(t)
-    tokens.finish()
-
-    def others(j, carry):
-        multiply(lax.rem(t + j, tensor_size))
-        return carry
-
-    lax.fori_loop(1, tensor_size, others, 0)
-    for plane, dp in planes:
-        plane.forward()
+    tokens.finish(diagonal=False)
+    for jx in range(1, nx):
+        multiply(near(jx, 0))
+    for jy in range(1, ny):
+        multiply(near(0, jy))
+    for s in range(1, nz):
+        pass_on("o", o_place, s)
+        for way, *_ in links:
+            spread(s, way)
+    tokens.finish(diagonal=True)
+    for jx in range(1, nx):
+        for jy in range(1, ny):
+            multiply(near(jx, jy))
+
+    def between(i):
+        for s in range(nz):
+            if i == (tensor_size if s == nz - 1 else s * tensor_size // nz):
+                for plane, _ in groups[s]:
+                    plane.forward()
+
     attend(
         (tensor_size, heads_dev, kv_count, heads_dev * tensor_size, k_share),
         copies,
+        between,
         qkv,
         q_gain,
         k_gain,
@@ -303,18 +321,22 @@
         att,
         local_sem,
     )
-    column_slots = [copies.slot() for _ in planes]
-    for slot, (plane, dp) in zip(column_slots, planes):
-        plane.finish()
-        copies.send(slot, full.at[dp], full.at[dp], partner)
-    for step, slot in enumerate(column_slots):
-        dp = lax.rem(z + step, nz) * CORES + 1 - c
-        copies.receive(slot, full.at[dp], partner)
+    column_slots = {}
+    for group in groups:
+        for plane, step in group:
+            plane.finish()
+            column_slots[step] = copies.slot()
+            column = full.at[jnp.clip(d - step * CORES, 0, nz * CORES - 1)]
+            copies.send(column_slots[step], column, column, partner, plane.when)
+    for group in groups:
+        for plane, step in group:
+            column = full.at[jnp.clip(z - step, 0, nz - 1) * CORES + 1 - c]
+            copies.receive(column_slots[step], column, partner, plane.when)
     copies.finish()
 
 
 def attend(
-    plan, copies, qkv, q_gain, k_gain, kv_first, out, sums, q_bf, k_bf, v_bf, att, local_sem
+    plan, copies, between, qkv, q_gain, k_gain, kv_first, out, sums, q_bf, k_bf, v_bf, att, local_sem
 ):
     tensor_size, heads_dev, kv_count, heads_all, k_share = plan
     t, d = lax.axis_index("tensor"), lax.axis_index("dp")
@@ -377,6 +399,7 @@
 
     back = [copies.slot() for _ in range(tensor_size)]
     for i in range(tensor_size):
+        between(i)
         block, seen = slice(i * rows, (i + 1) * rows), (i + 1) * rows
         rows_idx = lax.broadcasted_iota(jnp.int32, (rows, seen), 0) + i * rows
         cols_idx = lax.broadcasted_iota(jnp.int32, (rows, seen), 1)
@@ -411,6 +434,7 @@
         att.at[pl.ds(pl.multiple_of(t * rows, 8), rows), :], columns(t), local_sem.at[0]
     )
     mine.start()
+    between(tensor_size)
     mine.wait()
     for j in range(1, tensor_size):
         copies.receive(back[j], columns(lax.rem(t - j + tensor_size, tensor_size)), at(j))
@@ -461,7 +485,7 @@
     bf16 = jnp.bfloat16
 
     per_plane = (nx - 1) + (ny - 1) + nx * (ny - 1) + ny * (nx - 1)
-    slots = 4 * (nz - 1) + (nz + 1) * per_plane + 2 * (2 * nz - 1) + nz + 2 * tensor_size
+    slots = 4 * (nz - 1) + 2 * nz * per_plane + 2 * (2 * nz - 1) + 2 * tensor_size
     o_full, attended = pl.pallas_call(
         functools.partial(
             layer_kernel, (ny, nx, nz, heads_dev, kv_count, group_size, k_share)

time: 168 us -> 165 us (0.982)
  the two profiles are of different devices: /device:TPU:0 before, /device:TPU:21 now
where the time goes in v3:
time: 165 us
  Pallas kernels  165 us (100%)
    pallas_call x1, Pallas kernels, local(): pl.pallas_call(functools.partial(layer_kernel, (ny, nx, nz, heads_dev, kv...  152 us
    pallas_call x1, Pallas kernels, local(): pl.pallas_call(project_kernel, out_shape=jax.ShapeDtypeStruct((rows, mode...  12.9 us

profile of v3, /device:TPU:21, one launch (start us, length us, event | category | flops | bytes accessed | tf_op | source)
XLA Modules:
  0.0 164.9 jit_solution(5585681755679267030)
XLA Ops:
  0.0 152.0 %layer.1 = (bf16[8,1024,640]{2,1,0:T(8,128)(2,1)}, bf16[256,1024]{1,0:T(8,128)(2,1)}) custom-call(bf16[256,5120]{1,0:T(8,128)(2,1)} %hid.3, bf16[640,256]{1,0:T(8,128)(2,1)} %qw.1, bf16[640,1024]{1,0:T(8,128)(2,1)} %kw.1, bf16[640,1024]{1,0:T(8,128)(2,1)} %vw.1, bf16[256,640]{1,0:T(8,128)(2,1)} %ow.1, f32[1,256]{1,0:T(1,128)} %bitcast.5, f32[1,1024]{1,0:T(1,128)} %bitcast.4), custom_call_target="tpu_custom_call" | custom-call | tf_op jit(solution)/shard_map/layer/pallas_call | solution.py:489
  152.0 12.9 %project.1 = bf16[256,5120]{1,0:T(8,128)(2,1)} custom-call(bf16[256,1024]{1,0:T(8,128)(2,1)} %get-tuple-element.7.att, bf16[8,1024,640]{2,1,0:T(8,128)(2,1)} %get-tuple-element.8.weight, bf16[256,5120]{1,0:T(8,128)(2,1)} %hid.3, f32[1,5120]{1,0:T(1,128)} %bitcast.3), custom_call_target="tpu_custom_call" | custom-call | tf_op jit(solution)/shard_map/project/pallas_call | solution.py:517

commit v4 on v3

--- a/solution.py
+++ b/solution.py
@@ -292,12 +292,15 @@
         multiply(near(0, jy))
     for s in range(1, nz):
         pass_on("o", o_place, s)
-        for way, *_ in links:
-            spread(s, way)
     tokens.finish(diagonal=True)
     for jx in range(1, nx):
         for jy in range(1, ny):
             multiply(near(jx, jy))
+
+    def sums_sent():
+        for s in range(1, nz):
+            for way, *_ in links:
+                spread(s, way)
 
     def between(i):
         for s in range(nz):
@@ -305,9 +308,10 @@
                 for plane, _ in groups[s]:
                     plane.forward()
 
-    attend(
+    arrived = attend(
         (tensor_size, heads_dev, kv_count, heads_dev * tensor_size, k_share),
         copies,
+        sums_sent,
         between,
         qkv,
         q_gain,
@@ -332,11 +336,26 @@
         for plane, step in group:
             column = full.at[jnp.clip(z - step, 0, nz - 1) * CORES + 1 - c]
             copies.receive(column_slots[step], column, partner, plane.when)
+    arrived()
     copies.finish()
 
 
 def attend(
-    plan, copies, between, qkv, q_gain, k_gain, kv_first, out, sums, q_bf, k_bf, v_bf, att, local_sem
+    plan,
+    copies,
+    sums_sent,
+    between,
+    qkv,
+    q_gain,
+    k_gain,
+    kv_first,
+    out,
+    sums,
+    q_bf,
+    k_bf,
+    v_bf,
+    att,
+    local_sem,
 ):
     tensor_size, heads_dev, kv_count, heads_all, k_share = plan
     t, d = lax.axis_index("tensor"), lax.axis_index("dp")
@@ -366,6 +385,7 @@
     slots = [copies.slot() for _ in range(1, tensor_size)]
     for j in range(1, tensor_size):
         copies.send(slots[j - 1], sums.at[0], sums.at[j], at(j))
+    sums_sent()
     v_bf[...] = qkv[:, q_width + kv_width :].astype(jnp.bfloat16)
     for j in range(1, tensor_size):
         copies.receive(slots[j - 1], sums.at[j], at(j))
@@ -436,8 +456,12 @@
     mine.start()
     between(tensor_size)
     mine.wait()
-    for j in range(1, tensor_size):
-        copies.receive(back[j], columns(lax.rem(t - j + tensor_size, tensor_size)), at(j))
+
+    def arrived():
+        for j in range(1, tensor_size):
+            copies.receive(back[j], columns(lax.rem(t - j + tensor_size, tensor_size)), at(j))
+
+    return arrived
 
 
 def project_kernel(att, weight, hid, gain, out, projected, squares):

time: 165 us -> 158 us (0.958)
  the two profiles are of different devices: /device:TPU:21 before, /device:TPU:0 now
where the time goes in v4:
time: 158 us
  Pallas kernels  158 us (100%)
    pallas_call x1, Pallas kernels, local(): pl.pallas_call(functools.partial(layer_kernel, (ny, nx, nz, heads_dev, kv...  145 us
    pallas_call x1, Pallas kernels, local(): pl.pallas_call(project_kernel, out_shape=jax.ShapeDtypeStruct((rows, mode...  12.9 us

profile of v4, /device:TPU:0, one launch (start us, length us, event | category | flops | bytes accessed | tf_op | source)
XLA Modules:
  0.0 157.6 jit_solution(5041956166623513827)
XLA Ops:
  0.0 144.6 %layer.1 = (bf16[8,1024,640]{2,1,0:T(8,128)(2,1)}, bf16[256,1024]{1,0:T(8,128)(2,1)}) custom-call(bf16[256,5120]{1,0:T(8,128)(2,1)} %hid.3, bf16[640,256]{1,0:T(8,128)(2,1)} %qw.1, bf16[640,1024]{1,0:T(8,128)(2,1)} %kw.1, bf16[640,1024]{1,0:T(8,128)(2,1)} %vw.1, bf16[256,640]{1,0:T(8,128)(2,1)} %ow.1, f32[1,256]{1,0:T(1,128)} %bitcast.5, f32[1,1024]{1,0:T(1,128)} %bitcast.4), custom_call_target="tpu_custom_call" | custom-call | tf_op jit(solution)/shard_map/layer/pallas_call | solution.py:513
  144.6 12.9 %project.1 = bf16[256,5120]{1,0:T(8,128)(2,1)} custom-call(bf16[256,1024]{1,0:T(8,128)(2,1)} %get-tuple-element.7.att, bf16[8,1024,640]{2,1,0:T(8,128)(2,1)} %get-tuple-element.8.weight, bf16[256,5120]{1,0:T(8,128)(2,1)} %hid.3, f32[1,5120]{1,0:T(1,128)} %bitcast.3), custom_call_target="tpu_custom_call" | custom-call | tf_op jit(solution)/shard_map/project/pallas_call | solution.py:541

commit v5 on v4

--- a/solution.py
+++ b/solution.py
@@ -467,9 +467,12 @@
 def project_kernel(att, weight, hid, gain, out, projected, squares):
     n = pl.program_id(0)
     blocks, _, cols = projected.shape
-    block = jnp.dot(att[...], weight[0], preferred_element_type=jnp.float32)
-    projected[n] = block
-    here = jnp.sum(block * block, axis=1, keepdims=True)
+    each = weight.shape[0]
+    here = 0.0
+    for b in range(each):
+        block = jnp.dot(att[...], weight[b], preferred_element_type=jnp.float32)
+        projected[n * each + b] = block
+        here = here + jnp.sum(block * block, axis=1, keepdims=True)
 
     @pl.when(n == 0)
     def _():
@@ -479,7 +482,7 @@
     def _():
         squares[...] += here
 
-    @pl.when(n == blocks - 1)
+    @pl.when(n == blocks // each - 1)
     def _():
         scale = lax.rsqrt(squares[...] / (blocks * cols) + epsilon)
         for b in range(blocks):
@@ -541,10 +544,10 @@
     return pl.pallas_call(
         project_kernel,
         out_shape=jax.ShapeDtypeStruct((rows, model), bf16),
-        grid=(dp_size,),
+        grid=(dp_size // CORES,),
         in_specs=[
             pl.BlockSpec(attended.shape, lambda n: (0, 0)),
-            pl.BlockSpec((1,) + o_full.shape[1:], lambda n: (n, 0, 0)),
+            pl.BlockSpec((CORES,) + o_full.shape[1:], lambda n: (n, 0, 0)),
             pl.BlockSpec((rows, model), lambda n: (0, 0)),
             pl.BlockSpec((1, model), lambda n: (0, 0)),
         ],

time: 158 us -> 156 us (0.987)
  Pallas kernels: 158 us -> 155 us
    pallas_call x1, Pallas kernels: 12.9 us -> 10.8 us  [local(): pl.pallas_call(project_kernel, out_shape=jax.ShapeDtypeStruct((rows, mode...]
where the time goes in v5:
time: 156 us; the launch traced here: 155 us
  Pallas kernels  155 us (99%)
    pallas_call x1, Pallas kernels, local(): pl.pallas_call(functools.partial(layer_kernel, (ny, nx, nz, heads_dev, kv...  145 us
    pallas_call x1, Pallas kernels, local(): pl.pallas_call(project_kernel, out_shape=jax.ShapeDtypeStruct((rows, mode...  10.8 us

profile of v5, /device:TPU:0, one launch (start us, length us, event | category | flops | bytes accessed | tf_op | source)
XLA Modules:
  0.0 155.5 jit_solution(541122490970047960)
XLA Ops:
  0.0 144.6 %layer.1 = (bf16[8,1024,640]{2,1,0:T(8,128)(2,1)}, bf16[256,1024]{1,0:T(8,128)(2,1)}) custom-call(bf16[256,5120]{1,0:T(8,128)(2,1)} %hid.3, bf16[640,256]{1,0:T(8,128)(2,1)} %qw.1, bf16[640,1024]{1,0:T(8,128)(2,1)} %kw.1, bf16[640,1024]{1,0:T(8,128)(2,1)} %vw.1, bf16[256,640]{1,0:T(8,128)(2,1)} %ow.1, f32[1,256]{1,0:T(1,128)} %bitcast.5, f32[1,1024]{1,0:T(1,128)} %bitcast.4), custom_call_target="tpu_custom_call" | custom-call | tf_op jit(solution)/shard_map/layer/pallas_call | solution.py:516
  144.6 10.8 %project.1 = bf16[256,5120]{1,0:T(8,128)(2,1)} custom-call(bf16[256,1024]{1,0:T(8,128)(2,1)} %get-tuple-element.7.att, bf16[8,1024,640]{2,1,0:T(8,128)(2,1)} %get-tuple-element.8.weight, bf16[256,5120]{1,0:T(8,128)(2,1)} %hid.3, f32[1,5120]{1,0:T(1,128)} %bitcast.3), custom_call_target="tpu_custom_call" | custom-call | tf_op jit(solution)/shard_map/project/pallas_call | solution.py:544
